TPU v7x, 32 devices: a whole 2x2x4 slice. The times are simulated.
32 devices in a mesh: lat: 8 (over z, y), ch: 4 (over x, core).
Axes of the slice: x: 2, y: 2, z: 4, core: 2. Of those that a mesh axis runs over, the one named last changes fastest.
Arguments:
- state: float32 [1, 24, 180, 768], P(None, 'lat', None, 'ch'), may hold values from -30 to 30
- norm_gains: bfloat16 [2, 768], P(None, 'ch'), may hold values from 0.099609375 to 1.8984375
- channel_biases: bfloat16 [3, 768], P(None, 'ch'), may hold values from -2 to 2
- filter_in: float32 [2, 8, 96, 96], P(None, 'ch'), may hold values from -0.4375 to 0.4375
- filter_in_bias: float32 [2, 8, 96], P(None, 'ch'), may hold values from -2 to 2
- filter_out: float32 [2, 8, 96, 96], P(None, 'ch'), may hold values from -0.4375 to 0.4375
- filter_out_bias: float32 [2, 8, 96], P(None, 'ch'), may hold values from -2 to 2
- up_weight: bfloat16 [768, 3072], P(None, 'ch'), may hold values from -0.21875 to 0.21875
- up_bias: bfloat16 [3072], P('ch'), may hold values from -2 to 2
- down_weight: bfloat16 [3072, 768], P('ch'), may hold values from -0.109375 to 0.109375
Outputs:
- final_state: float32 [1, 24, 180, 768], P(None, 'lat', None, 'ch')
All inputs are finite; a program needn't handle non-finite values.
Results may differ from a plain program's by a relative error of at most 0.0012.
Values may be sent and summed in bfloat16 or wider, within the bound.
A program may use at most 128 MiB of HBM per device.

v0:
```python
import functools
import math

import jax
import jax.numpy as jnp
from jax import lax
import numpy as np
from jax.experimental import pallas as pl
from jax.experimental.pallas import tpu as pltpu
from jax.sharding import PartitionSpec as P

D = 768
M = 64
STEPS = 4


EPS = 1e-05
SHRINK = 0.01
HIGH = lax.Precision.HIGHEST


def longitude_tables(width, modes):
    column = jnp.arange(width, dtype=jnp.int32)[:, None]
    order = jnp.arange(modes, dtype=jnp.int32)[None, :]
    angle = 2.0 * math.pi / width * (column * order % width).astype(jnp.float32)
    doubled = jnp.where(order == 0, 1.0, 2.0).astype(jnp.float32)
    return (jnp.cos(angle), jnp.sin(angle), jnp.cos(angle) * doubled, jnp.sin(angle) * doubled)


def latitude_tables(height):
    column = jnp.arange(height, dtype=jnp.int32)[:, None]
    order = jnp.arange(height, dtype=jnp.int32)[None, :]
    angle = 2.0 * math.pi / height * (column * order % height).astype(jnp.float32)
    return (jnp.cos(angle), jnp.sin(angle))


def layer_norm(values, gain, shift):
    mean = jnp.sum(values, -1, keepdims=True) / values.shape[-1]
    spread = jnp.sum(values * values, -1, keepdims=True) / values.shape[-1] - mean * mean
    return (values - mean) * lax.rsqrt(spread + EPS) * gain + shift


def soft_shrink(values):
    return jnp.where(
        values > SHRINK, values - SHRINK, jnp.where(values < -SHRINK, values + SHRINK, 0.0)
    )


def block_apply(left, matrix):
    return jnp.einsum("bkmnj,nji->bkmni", left, matrix, precision=HIGH)


def spectral_mlp(real_part, imag_part, filter_in, filter_in_bias, filter_out, filter_out_bias):
    shape = real_part.shape
    blocks = filter_in.shape[1]
    size = filter_in.shape[2]
    real_blocks = real_part.reshape(shape[:-1] + (blocks, size))
    imag_blocks = imag_part.reshape(shape[:-1] + (blocks, size))
    first_real = jax.nn.relu(
        block_apply(real_blocks, filter_in[0])
        - block_apply(imag_blocks, filter_in[1])
        + filter_in_bias[0]
    )
    first_imag = jax.nn.relu(
        block_apply(imag_blocks, filter_in[0])
        + block_apply(real_blocks, filter_in[1])
        + filter_in_bias[1]
    )
    second_real = (
        block_apply(first_real, filter_out[0])
        - block_apply(first_imag, filter_out[1])
        + filter_out_bias[0]
    )
    second_imag = (
        block_apply(first_imag, filter_out[0])
        + block_apply(first_real, filter_out[1])
        + filter_out_bias[1]
    )
    return (soft_shrink(second_real).reshape(shape), soft_shrink(second_imag).reshape(shape))


def local(
    state,
    norm_gains,
    channel_biases,
    filter_in,
    filter_in_bias,
    filter_out,
    filter_out_bias,
    up_weight,
    up_bias,
    down_weight,
):
    width = state.shape[2]
    height = state.shape[1] * lax.axis_size("lat")
    scale = 1.0 / math.sqrt(height * width)
    lon_cos, lon_sin, back_cos, back_sin = longitude_tables(width, M)
    lat_cos, lat_sin = latitude_tables(height)
    gains = norm_gains.astype(jnp.float32)
    shifts = channel_biases.astype(jnp.float32)
    full_up, full_gains, full_biases = (
        lax.all_gather(up_weight, "ch", axis=1, tiled=True),
        lax.all_gather(norm_gains, "ch", axis=1, tiled=True),
        lax.all_gather(channel_biases, "ch", axis=1, tiled=True),
    )
    full_down, full_up_bias = (
        lax.all_gather(down_weight, "ch", axis=0, tiled=True),
        lax.all_gather(up_bias, "ch", axis=0, tiled=True),
    )
    wide_gains = full_gains.astype(jnp.float32)
    wide_biases = full_biases.astype(jnp.float32)
    wide_up_bias = full_up_bias.astype(jnp.float32)
    values = state
    for step_index in range(STEPS):
        total, squares = lax.psum(
            (jnp.sum(values, -1, keepdims=True), jnp.sum(values * values, -1, keepdims=True)), "ch"
        )
        mean = total / D
        mean, spread = (mean, squares / D - mean * mean)
        normed = (values - mean) * lax.rsqrt(spread + EPS) * gains[0] + shifts[0]
        real_lon = jnp.einsum("bhwd,wm->bhmd", normed, lon_cos, precision=HIGH)
        imag_lon = -jnp.einsum("bhwd,wm->bhmd", normed, lon_sin, precision=HIGH)
        stacked = lax.all_to_all(
            jnp.stack((real_lon, imag_lon)), "lat", split_axis=3, concat_axis=2, tiled=True
        )
        spectral_real_lon = stacked[0]
        spectral_imag_lon = stacked[1]
        real_spec = (
            jnp.einsum("kh,bhmd->bkmd", lat_cos, spectral_real_lon, precision=HIGH)
            + jnp.einsum("kh,bhmd->bkmd", lat_sin, spectral_imag_lon, precision=HIGH)
        ) * scale
        imag_spec = (
            jnp.einsum("kh,bhmd->bkmd", lat_cos, spectral_imag_lon, precision=HIGH)
            - jnp.einsum("kh,bhmd->bkmd", lat_sin, spectral_real_lon, precision=HIGH)
        ) * scale
        out_real, out_imag = spectral_mlp(
            real_spec, imag_spec, filter_in, filter_in_bias, filter_out, filter_out_bias
        )
        real_rows = jnp.einsum("kh,bkmd->bhmd", lat_cos, out_real, precision=HIGH) - jnp.einsum(
            "kh,bkmd->bhmd", lat_sin, out_imag, precision=HIGH
        )
        imag_rows = jnp.einsum("kh,bkmd->bhmd", lat_cos, out_imag, precision=HIGH) + jnp.einsum(
            "kh,bkmd->bhmd", lat_sin, out_real, precision=HIGH
        )
        rows = lax.all_to_all(
            jnp.stack((real_rows, imag_rows)), "lat", split_axis=2, concat_axis=3, tiled=True
        )
        back = jnp.einsum("bhmd,wm->bhwd", rows[0], back_cos, precision=HIGH) - jnp.einsum(
            "bhmd,wm->bhwd", rows[1], back_sin, precision=HIGH
        )
        values = values + back * scale + normed
        owned = lax.all_to_all(values, "ch", split_axis=2, concat_axis=3, tiled=True)
        normed_two = layer_norm(owned, wide_gains[1], wide_biases[1]).astype(jnp.bfloat16)
        flat = normed_two.reshape(-1, normed_two.shape[-1])
        pre = jnp.dot(flat, full_up, preferred_element_type=jnp.float32) + wide_up_bias
        hidden = jax.nn.gelu(pre, approximate=False).astype(jnp.bfloat16)
        mixed = jnp.dot(hidden, full_down, preferred_element_type=jnp.float32) + wide_biases[2]
        values = values + lax.all_to_all(
            mixed.reshape(owned.shape), "ch", split_axis=3, concat_axis=2, tiled=True
        )
    return values


F32 = jnp.float32
BF16 = jnp.bfloat16
MESH = pl.DeviceIdType.MESH


def split_table(table):
    high = np.asarray(table, np.float32).astype(jnp.bfloat16)
    low = (table - high.astype(np.float64)).astype(np.float32).astype(jnp.bfloat16)
    return np.stack((high, low))


def fourier_tables(width, part, height, modes, owners):
    scale = 1.0 / math.sqrt(height * width)
    share = modes // owners
    rows = height // owners
    half = -(-width // 2)
    token = np.arange(width)
    place = token // half * part + token % half
    order = np.arange(modes).reshape(owners, share)
    angle = 2.0 * np.pi / width * (order[:, :, None] * token % width)
    forward = np.zeros((owners, 2, share, 2 * part))
    forward[:, 0, :, place] = np.moveaxis(np.cos(angle), -1, 0)
    forward[:, 1, :, place] = np.moveaxis(-np.sin(angle), -1, 0)
    doubled = np.where(order == 0, 1.0, 2.0)[:, None, :, None] * scale
    backward = (forward * doubled).reshape(2 * modes, 2 * part).T
    forward = forward.reshape(2 * modes, 2 * part)
    turns = np.arange(height)
    turn = 2.0 * np.pi / height * (turns[:, None] * turns[None, :] % height)
    cos, sin, eye = np.cos(turn), np.sin(turn), np.eye(share)
    mix = np.array([[cos, sin], [-sin, cos]])
    size = 2 * height * share
    lat = np.einsum("abkh,mn->akmhbn", mix, eye).reshape(size, size) * scale
    unmix = np.array([[cos, -sin], [sin, cos]])
    back = np.einsum("bahk,mn->hbmakn", unmix, eye)
    back = back.reshape((owners, rows) + back.shape[1:]).swapaxes(0, 1).reshape(size, size)
    return tuple(split_table(t) for t in (forward, lat, back, backward))


def dot(left, right):
    return jnp.dot(left, right, preferred_element_type=F32)


def halves(values):
    high = values.astype(BF16)
    return high, (values - high.astype(F32)).astype(BF16)


def dot3(left, right):
    return dot(left[0], right[0]) + dot(left[1], right[0]) + dot(left[0], right[1])


def gelu(values):
    return 0.5 * values * (1.0 + lax.erf(values * (1.0 / math.sqrt(2.0))))


def flip(index, bits):
    bit, moved = 1, index
    while bit <= bits:
        if bits & bit:
            moved = moved + bit - 2 * bit * lax.rem(lax.div(index, bit), 2)
        bit *= 2
    return moved


STAT, LON, ROW, STAT2, TOK, MIX, SETUP = range(7)


def rollout(
    lats,
    chans,
    state,
    gains,
    shifts,
    fin_bias,
    fout_bias,
    up_bias,
    fin_hbm,
    fout_hbm,
    up_hbm,
    down_hbm,
    t_lon_hbm,
    t_lat_hbm,
    t_rows_hbm,
    t_back_hbm,
    out,
    x,
    stat_send,
    stat_recv,
    lon_send,
    lon_recv,
    row_send,
    row_recv,
    tok_send,
    tok_recv,
    mix_full,
    mix_send,
    mix_pair,
    mix_recv,
    bias_send,
    bias_recv,
    fin_raw,
    fout_raw,
    fin,
    fout,
    fin_b,
    fout_b,
    up,
    down,
    up_recv,
    down_recv,
    t_lon,
    t_lat,
    t_rows,
    t_back,
    hidden,
    load_sem,
    send_sem,
    recv_sem,
):
    lat, ch = lax.axis_index("lat"), lax.axis_index("ch")
    core, chip = lax.rem(ch, 2), lax.div(ch, 2)
    chips = chans // 2
    rows, width, own = state.shape
    part = x.shape[2]
    near = -(-width // 2)
    wide = chans * own
    hid = up.shape[1]
    spread_modes = t_lon.shape[1]

    def chan(q):
        return 2 * lax.rem(chip + q // 2, chips) + (core if q % 2 == 0 else 1 - core)

    def half_of(q):
        return core if q % 2 == 0 else 1 - core

    lat_order = sorted(range(1, lats), reverse=True)
    ch_order = tuple(range(2, chans)) + (1,)

    loads = [
        pltpu.make_async_copy(source, target, load_sem.at[n])
        for n, (source, target) in enumerate(
            (
                (fin_hbm, fin_raw),
                (fout_hbm, fout_raw),
                (t_lon_hbm, t_lon),
                (t_lat_hbm, t_lat),
                (t_rows_hbm, t_rows),
                (t_back_hbm, t_back),
                (up_hbm, up),
                (down_hbm, down),
            )
        )
    ]
    for each in loads:
        each.start()

    barrier = pltpu.get_barrier_semaphore()
    for k in lat_order:
        pl.semaphore_signal(barrier, inc=1, device_id={"lat": flip(lat, k)}, device_id_type=MESH)
    for q in ch_order:
        pl.semaphore_signal(barrier, inc=1, device_id={"ch": chan(q)}, device_id_type=MESH)

    def copy(kind, r, k, source, target, device):
        return pltpu.make_async_remote_copy(
            src_ref=source,
            dst_ref=target,
            send_sem=send_sem.at[kind, r, k],
            recv_sem=recv_sem.at[kind, r, k],
            device_id=device,
            device_id_type=MESH,
        )

    def stat_copies(kind, r):
        n = kind // STAT2
        return [
            copy(kind, r, q, stat_send.at[n, r], stat_recv.at[n, r, ch], {"ch": chan(q)})
            for q in ch_order
        ]

    def lon_copies(r):
        return [
            copy(LON, r, k, lon_send.at[r, flip(lat, k)], lon_recv.at[lat, r], {"lat": flip(lat, k)})
            for k in lat_order
        ]

    def row_copies(r):
        return [
            copy(ROW, r, k, row_send.at[r, flip(lat, k)], row_recv.at[r, lat], {"lat": flip(lat, k)})
            for k in lat_order
        ]

    def tok_copies(r):
        return [
            copy(TOK, r, q, tok_send.at[r, half_of(q)], tok_recv.at[r, ch], {"ch": chan(q)})
            for q in ch_order
        ]

    def mix_copies(r):
        copies = [
            copy(MIX, r, q, mix_send.at[r, chan(q)], mix_recv.at[r, q // 2 - 1, core], {"ch": chan(q)})
            for q in range(2, chans)
        ]
        copies.append(copy(MIX, r, 1, mix_full.at[r, chan(1)], mix_pair.at[r], {"ch": chan(1)}))
        return copies

    def start(copies):
        for each in copies:
            each.start()

    def finish(copies):
        for each in copies:
            each.wait()

    gain = gains[...].astype(F32)
    shift = shifts[...].astype(F32)
    bias_send[...] = jnp.broadcast_to(up_bias[...].astype(F32), bias_send.shape)
    x[...] = jnp.zeros_like(x)
    for r in range(rows):
        x[r, 0, 0:near] = state[r, 0:near]
        x[r, 1, 0 : width - near] = state[r, near:width]
    ones = jnp.ones((8, own), BF16)
    which = lax.broadcasted_iota(jnp.int32, (8, 2 * part), 0)

    def row_sums(values):
        dims = (((1,), (1,)), ((), ()))
        high, low = halves(values)
        return lax.dot_general(
            ones, high, dims, preferred_element_type=F32
        ) + lax.dot_general(ones, low, dims, preferred_element_type=F32)

    def send_stats(kind, r):
        n = kind // STAT2
        values = x[r].reshape(2 * part, own)
        sums = jnp.where(which == 0, row_sums(values), row_sums(values * values))
        stat_send[n, r] = sums
        stat_recv[n, r, pl.ds(ch, 1)] = sums[None]
        start(stat_copies(kind, r))

    def take_stats(kind, r):
        n = kind // STAT2
        finish(stat_copies(kind, r))
        total = stat_recv[n, r, 0]
        for c in range(1, chans):
            total = total + stat_recv[n, r, c]
        mean = total[0:1] / wide
        scaled = lax.rsqrt(total[1:2] / wide - mean * mean + EPS)
        both = jnp.transpose(jnp.where(which == 0, mean, scaled))
        return both[:, 0:1], both[:, 1:2]

    pl.semaphore_wait(barrier, lats + chans - 2)
    for r in range(rows):
        send_stats(STAT, r)
    partner = {"ch": chan(1)}
    setup = [
        copy(SETUP, 0, 0, up_hbm, up_recv, partner),
        copy(SETUP, 0, 1, down_hbm, down_recv, partner),
        copy(SETUP, 0, 2, bias_send, bias_recv, partner),
    ]
    start(setup)
    loads[0].wait()
    loads[1].wait()
    blocks, size = fin_raw.shape[1], fin_raw.shape[2]
    line = lax.broadcasted_iota(jnp.int32, (size, own), 0)
    lane = lax.broadcasted_iota(jnp.int32, (size, own), 1)
    for raw, target, bias, bias_target in (
        (fin_raw, fin, fin_bias, fin_b),
        (fout_raw, fout, fout_bias, fout_b),
    ):
        placed = 0.0
        for n in range(blocks):
            shifted = jnp.where(lane == line + n * size, 1.0, 0.0)
            select = shifted.astype(BF16)
            for p in range(2):
                high, low = halves(raw[p, n])
                target[p, 0, n * size : (n + 1) * size] = dot(high, select).astype(BF16)
                target[p, 1, n * size : (n + 1) * size] = dot(low, select).astype(BF16)
            placed = placed + jnp.dot(
                bias[:, n, :], shifted, precision=HIGH, preferred_element_type=F32
            )
        bias_target[...] = placed
    for each in loads[2:6]:
        each.wait()

    def complex_apply(pair, weights, bias):
        split = pair.shape[0] // 2
        pair = halves(pair)
        one = dot3(pair, (weights[0, 0], weights[0, 1]))
        two = dot3(pair, (weights[1, 0], weights[1, 1]))
        return (
            one[:split] - two[split:] + bias[0:1, :],
            one[split:] + two[:split] + bias[1:2, :],
        )

    @pl.loop(0, STEPS)
    def _(index):
        for r in range(rows):
            mean, scaled = take_stats(STAT, r)
            now = x[r].reshape(2 * part, own)
            normed = (now - mean) * scaled * gain[0:1] + shift[0:1]
            x[r] = (now + normed).reshape(2, part, own)
            spectra = dot3((t_lon[0], t_lon[1]), halves(normed))
            lon_send[r] = spectra.astype(BF16).reshape(lats, spread_modes // lats, own)
            start(lon_copies(r))
            lon_recv[pl.ds(lat, 1), r] = lon_send[r, pl.ds(lat, 1)]
        for r in range(rows):
            finish(lon_copies(r))
        data = lon_recv[...].reshape(-1, own)
        spec = dot(t_lat[0], data) + dot(t_lat[1], data)
        real, imag = complex_apply(spec, fin, fin_b)
        pair = jnp.concatenate((jnp.maximum(real, 0.0), jnp.maximum(imag, 0.0)), 0)
        real, imag = complex_apply(pair, fout, fout_b)
        pair = halves(jnp.concatenate((soft_shrink(real), soft_shrink(imag)), 0))
        for r in range(rows):
            cut = slice(r * spread_modes, (r + 1) * spread_modes)
            back = dot3((t_rows[0, cut], t_rows[1, cut]), pair)
            row_send[r] = back.astype(BF16).reshape(lats, spread_modes // lats, own)
            start(row_copies(r))
            row_recv[r, pl.ds(lat, 1)] = row_send[r, pl.ds(lat, 1)]
        for r in range(rows):
            finish(row_copies(r))
            data = row_recv[r].reshape(-1, own)
            back = dot(t_back[0], data) + dot(t_back[1], data)
            x[r] = x[r] + back.reshape(2, part, own)
            send_stats(STAT2, r)
        for r in range(rows):
            mean, scaled = take_stats(STAT2, r)
            now = x[r].reshape(2 * part, own)
            normed = (now - mean) * scaled * gain[1:2] + shift[1:2]
            tok_send[r] = normed.astype(BF16).reshape(2, part, own)
            start(tok_copies(r))
            tok_recv[r, pl.ds(ch, 1)] = tok_send[r, pl.ds(core, 1)]

        @pl.when(index == 0)
        def _():
            loads[6].wait()
            loads[7].wait()
            finish(setup)

        for r in range(rows):
            finish(tok_copies(r))
            for s, (weight, bias) in enumerate(((up, bias_send), (up_recv, bias_recv))):
                for lo in range(0, hid, 256):
                    cut = slice(lo, lo + 256)
                    pre = bias[0:1, cut]
                    for c in range(chans):
                        pre = pre + dot(tok_recv[r, c], weight[c * own : (c + 1) * own, cut])
                    hidden[s, :, cut] = gelu(pre).astype(BF16)
            mixed = dot(hidden[0], down[...]) + dot(hidden[1], down_recv[...])
            for c in range(chans):
                piece = mixed[:, c * own : (c + 1) * own]
                mix_full[r, c] = piece
                mix_send[r, c] = piece.astype(BF16)
            start(mix_copies(r))
        for r in range(rows):
            finish(mix_copies(r))
            for h, piece in ((core, mix_full[r, pl.ds(ch, 1)]), (1 - core, mix_pair[r][None])):
                for n in range(chips - 1):
                    piece = piece + mix_recv[r, n, pl.ds(h, 1)].astype(F32)
                x[r, pl.ds(h, 1)] = x[r, pl.ds(h, 1)] + piece + shift[2:3]

            @pl.when(index < STEPS - 1)
            def _():
                send_stats(STAT, r)

    for r in range(rows):
        out[r, 0:near] = x[r, 0, 0:near]
        out[r, near:width] = x[r, 1, 0 : width - near]


def fused(
    lats,
    chans,
    state,
    norm_gains,
    channel_biases,
    filter_in,
    filter_in_bias,
    filter_out,
    filter_out_bias,
    up_weight,
    up_bias,
    down_weight,
):
    _, rows, width, own = state.shape
    part = -(--(-width // 2) // 16) * 16
    share = 2 * M // lats
    hid = up_weight.shape[1]
    tables = tuple(
        jnp.asarray(t) for t in fourier_tables(width, part, rows * lats, M, lats)
    )
    args = (
        state[0],
        norm_gains,
        channel_biases,
        filter_in_bias,
        filter_out_bias,
        up_bias.reshape(1, hid),
        filter_in,
        filter_out,
        up_weight,
        down_weight,
    ) + tables
    vmem = pl.BlockSpec(memory_space=pltpu.VMEM)
    hbm = pl.BlockSpec(memory_space=pltpu.HBM)
    spectrum = (rows, lats, share, own)
    peers = max(lats, chans)
    result = pl.pallas_call(
        functools.partial(rollout, lats, chans),
        out_shape=jax.ShapeDtypeStruct((rows, width, own), F32),
        in_specs=[vmem] * 6 + [hbm] * 8,
        out_specs=vmem,
        scratch_shapes=[
            pltpu.VMEM((rows, 2, part, own), F32),
            pltpu.VMEM((2, rows, 8, 2 * part), F32),
            pltpu.VMEM((2, rows, chans, 8, 2 * part), F32),
            pltpu.VMEM(spectrum, BF16),
            pltpu.VMEM((lats, rows, share, own), BF16),
            pltpu.VMEM(spectrum, BF16),
            pltpu.VMEM(spectrum, BF16),
            pltpu.VMEM((rows, 2, part, own), BF16),
            pltpu.VMEM((rows, chans, part, own), BF16),
            pltpu.VMEM((rows, chans, part, own), F32),
            pltpu.VMEM((rows, chans, part, own), BF16),
            pltpu.VMEM((rows, part, own), F32),
            pltpu.VMEM((rows, chans // 2 - 1, 2, part, own), BF16),
            pltpu.VMEM((8, hid), F32),
            pltpu.VMEM((8, hid), F32),
            pltpu.VMEM(filter_in.shape, F32),
            pltpu.VMEM(filter_out.shape, F32),
            pltpu.VMEM((2, 2, own, own), BF16),
            pltpu.VMEM((2, 2, own, own), BF16),
            pltpu.VMEM((2, own), F32),
            pltpu.VMEM((2, own), F32),
            pltpu.VMEM(up_weight.shape, BF16),
            pltpu.VMEM(down_weight.shape, BF16),
            pltpu.VMEM(up_weight.shape, BF16),
            pltpu.VMEM(down_weight.shape, BF16),
        ]
        + [pltpu.VMEM(t.shape, BF16) for t in tables]
        + [
            pltpu.VMEM((2, part, hid), BF16),
            pltpu.SemaphoreType.DMA((8,)),
            pltpu.SemaphoreType.DMA((7, rows, peers)),
            pltpu.SemaphoreType.DMA((7, rows, peers)),
        ],
        compiler_params=pltpu.CompilerParams(
            collective_id=0, has_side_effects=True, vmem_limit_bytes=48 * 1024 * 1024
        ),
    )(*args)
    return result[None]


def dispatch(sizes, *args):
    lats, chans = sizes["lat"], sizes["ch"]
    if 2 * M // lats % 16 == 0 and chans > 2 and chans % 2 == 0:
        return fused(lats, chans, *args)
    return local(*args)


def solution(mesh):
    placed = (
        P(None, "lat", None, "ch"),
        P(None, "ch"),
        P(None, "ch"),
        P(None, "ch", None, None),
        P(None, "ch", None),
        P(None, "ch", None, None),
        P(None, "ch", None),
        P(None, "ch"),
        P("ch"),
        P("ch", None),
    )
    return jax.shard_map(
        functools.partial(dispatch, dict(mesh.shape)), mesh=mesh, in_specs=placed, out_specs=P(None, "lat", None, "ch"), check_vma=False
    )
```

profile of v0, /device:TPU:0, one launch (start us, length us, event | category | flops | bytes accessed | tf_op | source)
XLA Modules:
  0.0 151.9 jit_solution(8906269416943131464)
XLA Ops:
  0.0 0.0 copy-start.2
  0.0 0.0 copy-start.6
  0.0 0.0 copy-start.5
  0.0 0.0 copy-start.4
  0.0 0.8 reshape.3.up_bias
  0.8 1.1 copy.18
  1.9 0.0 copy-done.2
  1.9 0.0 copy-done.6
  1.9 0.0 copy-done.5
  1.9 0.0 copy-done.4
  1.9 0.0 copy-start
  1.9 1.3 copy-done
  3.2 0.0 copy-start.1
  3.2 1.3 copy-done.1
  4.5 0.0 copy-start.3
  4.5 1.1 copy-done.3
  5.5 0.0 copy-start.7
  5.5 0.9 copy-done.7
  6.4 0.0 copy-start.8
  6.4 0.7 copy-done.8
  7.1 0.0 copy-start.9
  7.1 0.7 copy-done.9
  7.8 0.0 copy-start.10
  7.8 0.7 copy-done.10
  8.5 0.0 copy-start.11
  8.5 0.7 copy-done.11
  9.2 141.4 %shard_map.136 = f32[3,180,192]{2,1,0:T(8,128)S(1)} custom-call(f32[3,180,192]{2,1,0:T(8,128)S(1)} %bitcast.5, bf16[2,192]{1,0:T(2,128)(2,1)S(1)} %copy-done.11, bf16[3,192]{1,0:T(4,128)(2,1)S(1)} %copy-done.8, f32[2,2,96]{2,1,0:T(2,128)S(1)} %copy-done.9, f32[2,2,96]{2,1,0:T(2,128)S(1)} %copy-done.10, bf16[1,768]{1,0:T(2,128)(2,1)S(1)} %reshape.3.up_bias, ...), custom_call_target="tpu_custom_call" | custom-call | tf_op jit(solution)/shard_map/pallas_call | solution.py:570
  150.5 1.4 copy.15
Async XLA Ops:
  0.0 1.9 %copy-start.2 = (bf16[2,384,384]{2,1,0:T(8,128)(2,1)S(1)}, bf16[2,384,384]{2,1,0:T(8,128)(2,1)}, u32[]{:S(2)}) copy-start(bf16[2,384,384]{2,1,0:T(8,128)(2,1)} %constant.10.clone.t_rows_hbm) | copy-start | bytes 1769476
  0.0 1.9 %copy-start.6 = (bf16[2,128,192]{2,1,0:T(8,128)(2,1)S(1)}, bf16[2,128,192]{2,1,0:T(8,128)(2,1)}, u32[]{:S(2)}) copy-start(bf16[2,128,192]{2,1,0:T(8,128)(2,1)} %constant.8.clone.t_lon_hbm) | copy-start | bytes 294916
  0.0 1.9 %copy-start.5 = (f32[2,2,96,96]{3,2,1,0:T(8,128)S(1)}, f32[2,2,96,96]{3,2,1,0:T(8,128)}, u32[]{:S(2)}) copy-start(f32[2,2,96,96]{3,2,1,0:T(8,128)} %fout_hbm.1) | copy-start | bytes 442372
  0.0 1.9 %copy-start.4 = (f32[2,2,96,96]{3,2,1,0:T(8,128)S(1)}, f32[2,2,96,96]{3,2,1,0:T(8,128)}, u32[]{:S(2)}) copy-start(f32[2,2,96,96]{3,2,1,0:T(8,128)} %fin_hbm.1) | copy-start | bytes 442372
  1.9 1.3 copy-start
  3.2 1.3 copy-start.1
  4.5 1.1 copy-start.3
  5.5 0.9 copy-start.7
  6.4 0.7 copy-start.8
  7.1 0.7 copy-start.9
  7.8 0.7 copy-start.10
  8.5 0.7 copy-start.11
where the time goes:
time: 152 us
  Pallas kernels  141 us (93%)
  local copies, waits for them, and re-layouts  10.5 us (7%)
    pallas_call x1, Pallas kernels, fused(): pl.pallas_call(functools.partial(rollout, lats, chans), out_shape=jax.Sha...  141 us
    unnamed x25, local copies, waits for them, and re-layouts  8.32 us

commit v1 on v0

--- a/solution.py
+++ b/solution.py
@@ -223,6 +223,28 @@
             moved = moved + bit - 2 * bit * lax.rem(lax.div(index, bit), 2)
         bit *= 2
     return moved
+
+
+LANES = 128
+
+
+def pack(values):
+    rows = values.shape[-2] // 2
+    rest = values[..., LANES:]
+    folded = jnp.concatenate((rest[..., :rows, :], rest[..., rows:, :]), -1)
+    return values[..., :LANES].astype(BF16), folded.astype(BF16)
+
+
+def unfold(folded):
+    values = folded.astype(F32)
+    return jnp.concatenate((values[..., : LANES // 2], values[..., LANES // 2 :]), -2)
+
+
+def store_packed(target, where, values):
+    rows = values.shape[-2]
+    full, folded = pack(values)
+    target[where + (slice(0, rows),)] = full
+    target[where + (slice(rows, rows + rows // 2),)] = folded
 
 
 STAT, LON, ROW, STAT2, TOK, MIX, SETUP = range(7)
@@ -275,6 +297,7 @@
     t_lat,
     t_rows,
     t_back,
+    tokens,
     hidden,
     load_sem,
     send_sem,
@@ -296,6 +319,12 @@
     def half_of(q):
         return core if q % 2 == 0 else 1 - core
 
+    up_rows = []
+    for c in range(chans):
+        up_rows.append((pl.ds(c * own, LANES), pl.ds(c * LANES, LANES)))
+        rest = own - LANES
+        up_rows.append((pl.ds(c * own + LANES, rest), pl.ds(chans * LANES + c * rest, rest)))
+
     lat_order = sorted(range(1, lats), reverse=True)
     ch_order = tuple(range(2, chans)) + (1,)
 
@@ -309,9 +338,9 @@
                 (t_lat_hbm, t_lat),
                 (t_rows_hbm, t_rows),
                 (t_back_hbm, t_back),
-                (up_hbm, up),
                 (down_hbm, down),
             )
+            + tuple((up_hbm.at[source], up.at[target]) for source, target in up_rows)
         )
     ]
     for each in loads:
@@ -401,7 +430,8 @@
 
     def take_stats(kind, r):
         n = kind // STAT2
-        finish(stat_copies(kind, r))
+        with jax.named_scope(f"wait_stat#n={n}"):
+            finish(stat_copies(kind, r))
         total = stat_recv[n, r, 0]
         for c in range(1, chans):
             total = total + stat_recv[n, r, c]
@@ -415,10 +445,13 @@
         send_stats(STAT, r)
     partner = {"ch": chan(1)}
     setup = [
-        copy(SETUP, 0, 0, up_hbm, up_recv, partner),
-        copy(SETUP, 0, 1, down_hbm, down_recv, partner),
-        copy(SETUP, 0, 2, bias_send, bias_recv, partner),
+        copy(SETUP, 0, 0, down_hbm, down_recv, partner),
+        copy(SETUP, 0, 1, bias_send, bias_recv, partner),
     ]
+    for n, (source, target) in enumerate(up_rows):
+        setup.append(
+            copy(SETUP, 1 + n // chans, n % chans, up_hbm.at[source], up_recv.at[target], partner)
+        )
     start(setup)
     loads[0].wait()
     loads[1].wait()
@@ -454,72 +487,133 @@
             one[split:] + two[:split] + bias[1:2, :],
         )
 
-    @pl.loop(0, STEPS)
-    def _(index):
-        for r in range(rows):
+    def spectrum(messages, count):
+        full = messages[..., :count, :]
+        rest = unfold(messages[..., count:, :]).astype(BF16)
+        return jnp.concatenate((full, rest), -1).reshape(-1, own)
+
+    share = spread_modes // lats
+
+    def forward(r):
+        with jax.named_scope("forward"):
             mean, scaled = take_stats(STAT, r)
             now = x[r].reshape(2 * part, own)
             normed = (now - mean) * scaled * gain[0:1] + shift[0:1]
             x[r] = (now + normed).reshape(2, part, own)
             spectra = dot3((t_lon[0], t_lon[1]), halves(normed))
-            lon_send[r] = spectra.astype(BF16).reshape(lats, spread_modes // lats, own)
+            store_packed(lon_send, (r, slice(None)), spectra.reshape(lats, share, own))
             start(lon_copies(r))
             lon_recv[pl.ds(lat, 1), r] = lon_send[r, pl.ds(lat, 1)]
-        for r in range(rows):
-            finish(lon_copies(r))
-        data = lon_recv[...].reshape(-1, own)
+
+    def spectral():
+        data = spectrum(lon_recv[...], share)
         spec = dot(t_lat[0], data) + dot(t_lat[1], data)
         real, imag = complex_apply(spec, fin, fin_b)
         pair = jnp.concatenate((jnp.maximum(real, 0.0), jnp.maximum(imag, 0.0)), 0)
         real, imag = complex_apply(pair, fout, fout_b)
-        pair = halves(jnp.concatenate((soft_shrink(real), soft_shrink(imag)), 0))
+        return halves(jnp.concatenate((soft_shrink(real), soft_shrink(imag)), 0))
+
+    def unmix(r, pair):
+        cut = slice(r * spread_modes, (r + 1) * spread_modes)
+        back = dot3((t_rows[0, cut], t_rows[1, cut]), pair)
+        store_packed(row_send, (r, slice(None)), back.reshape(lats, share, own))
+        start(row_copies(r))
+        row_recv[r, pl.ds(lat, 1)] = row_send[r, pl.ds(lat, 1)]
+
+    def backward(r):
+        data = spectrum(row_recv[r], share)
+        back = dot(t_back[0], data) + dot(t_back[1], data)
+        x[r] = x[r] + back.reshape(2, part, own)
+        send_stats(STAT2, r)
+
+    def token(r):
+        mean, scaled = take_stats(STAT2, r)
+        now = x[r].reshape(2 * part, own)
+        normed = (now - mean) * scaled * gain[1:2] + shift[1:2]
+        store_packed(tok_send, (r, slice(None)), normed.reshape(2, part, own))
+        start(tok_copies(r))
+        tok_recv[r, pl.ds(ch, 1)] = tok_send[r, pl.ds(core, 1)]
+
+    def project_up(r):
+        for c in range(chans):
+            tokens[:, c * LANES : (c + 1) * LANES] = tok_recv[r, c, 0:part]
+        middle = part // 2
+        for c in range(0, chans, 2):
+            cut = slice((chans + c // 2) * LANES, (chans + c // 2 + 1) * LANES)
+            one = tok_recv[r, c, part : part + middle]
+            two = tok_recv[r, c + 1, part : part + middle]
+            for n, lanes in enumerate((slice(0, LANES // 2), slice(LANES // 2, LANES))):
+                pair = jnp.concatenate((one[:, lanes], two[:, lanes]), -1)
+                tokens[n * middle : (n + 1) * middle, cut] = pair
+        for s, (weight, bias) in enumerate(((up, bias_send), (up_recv, bias_recv))):
+            for lo in range(0, hid, 256):
+                cut = slice(lo, lo + 256)
+                pre = dot(tokens[...], weight[:, cut]) + bias[0:1, cut]
+                hidden[s, :, cut] = gelu(pre).astype(BF16)
+
+    def project_down(r):
+        mixed = dot(hidden[0], down[...]) + dot(hidden[1], down_recv[...])
+        for c in range(chans):
+            piece = mixed[:, c * own : (c + 1) * own]
+            mix_full[r, c] = piece
+            store_packed(mix_send, (r, c), piece)
+        start(mix_copies(r))
+
+    def residual(r):
+        for h, piece in ((core, mix_full[r, pl.ds(ch, 1)]), (1 - core, mix_pair[r][None])):
+            for n in range(chips - 1):
+                message = mix_recv[r, n, pl.ds(h, 1)]
+                rest = unfold(message[:, part:])
+                piece = piece + jnp.concatenate((message[:, :part].astype(F32), rest), -1)
+            x[r, pl.ds(h, 1)] = x[r, pl.ds(h, 1)] + piece + shift[2:3]
+
+    forward(0)
+
+    @pl.loop(0, STEPS)
+    def _(index):
+        for r in range(1, rows):
+            forward(r)
+        with jax.named_scope("wait_lon"):
+            for r in range(rows):
+                finish(lon_copies(r))
+        with jax.named_scope("spectral"):
+            pair = spectral()
+        with jax.named_scope("unmix"):
+            for r in range(rows):
+                unmix(r, pair)
         for r in range(rows):
-            cut = slice(r * spread_modes, (r + 1) * spread_modes)
-            back = dot3((t_rows[0, cut], t_rows[1, cut]), pair)
-            row_send[r] = back.astype(BF16).reshape(lats, spread_modes // lats, own)
-            start(row_copies(r))
-            row_recv[r, pl.ds(lat, 1)] = row_send[r, pl.ds(lat, 1)]
+            with jax.named_scope("wait_row"):
+                finish(row_copies(r))
+            with jax.named_scope("backward"):
+                backward(r)
         for r in range(rows):
-            finish(row_copies(r))
-            data = row_recv[r].reshape(-1, own)
-            back = dot(t_back[0], data) + dot(t_back[1], data)
-            x[r] = x[r] + back.reshape(2, part, own)
-            send_stats(STAT2, r)
-        for r in range(rows):
-            mean, scaled = take_stats(STAT2, r)
-            now = x[r].reshape(2 * part, own)
-            normed = (now - mean) * scaled * gain[1:2] + shift[1:2]
-            tok_send[r] = normed.astype(BF16).reshape(2, part, own)
-            start(tok_copies(r))
-            tok_recv[r, pl.ds(ch, 1)] = tok_send[r, pl.ds(core, 1)]
+            with jax.named_scope("token"):
+                token(r)
 
         @pl.when(index == 0)
         def _():
-            loads[6].wait()
-            loads[7].wait()
+            for each in loads[6:]:
+                each.wait()
             finish(setup)
 
         for r in range(rows):
-            finish(tok_copies(r))
-            for s, (weight, bias) in enumerate(((up, bias_send), (up_recv, bias_recv))):
-                for lo in range(0, hid, 256):
-                    cut = slice(lo, lo + 256)
-                    pre = bias[0:1, cut]
-                    for c in range(chans):
-                        pre = pre + dot(tok_recv[r, c], weight[c * own : (c + 1) * own, cut])
-                    hidden[s, :, cut] = gelu(pre).astype(BF16)
-            mixed = dot(hidden[0], down[...]) + dot(hidden[1], down_recv[...])
-            for c in range(chans):
-                piece = mixed[:, c * own : (c + 1) * own]
-                mix_full[r, c] = piece
-                mix_send[r, c] = piece.astype(BF16)
-            start(mix_copies(r))
+            with jax.named_scope("wait_tok"):
+                finish(tok_copies(r))
+            with jax.named_scope("up"):
+                project_up(r)
+            with jax.named_scope("down"):
+                project_down(r)
         for r in range(rows):
-            finish(mix_copies(r))
-            for h, piece in ((core, mix_full[r, pl.ds(ch, 1)]), (1 - core, mix_pair[r][None])):
-                for n in range(chips - 1):
-                    piece = piece + mix_recv[r, n, pl.ds(h, 1)].astype(F32)
-                x[r, pl.ds(h, 1)] = x[r, pl.ds(h, 1)] + piece + shift[2:3]
+            if r == rows - 1:
+
+                @pl.when(index < STEPS - 1)
+                def _():
+                    forward(0)
+
+            with jax.named_scope("wait_mix"):
+                finish(mix_copies(r))
+            with jax.named_scope("residual"):
+                residual(r)
 
             @pl.when(index < STEPS - 1)
             def _():
@@ -565,7 +659,9 @@
     ) + tables
     vmem = pl.BlockSpec(memory_space=pltpu.VMEM)
     hbm = pl.BlockSpec(memory_space=pltpu.HBM)
-    spectrum = (rows, lats, share, own)
+    packed = share + share // 2
+    spectrum = (rows, lats, packed, LANES)
+    folded = part + part // 2
     peers = max(lats, chans)
     result = pl.pallas_call(
         functools.partial(rollout, lats, chans),
@@ -577,15 +673,15 @@
             pltpu.VMEM((2, rows, 8, 2 * part), F32),
             pltpu.VMEM((2, rows, chans, 8, 2 * part), F32),
             pltpu.VMEM(spectrum, BF16),
-            pltpu.VMEM((lats, rows, share, own), BF16),
+            pltpu.VMEM((lats, rows, packed, LANES), BF16),
             pltpu.VMEM(spectrum, BF16),
             pltpu.VMEM(spectrum, BF16),
-            pltpu.VMEM((rows, 2, part, own), BF16),
-            pltpu.VMEM((rows, chans, part, own), BF16),
+            pltpu.VMEM((rows, 2, folded, LANES), BF16),
+            pltpu.VMEM((rows, chans, folded, LANES), BF16),
             pltpu.VMEM((rows, chans, part, own), F32),
-            pltpu.VMEM((rows, chans, part, own), BF16),
+            pltpu.VMEM((rows, chans, folded, LANES), BF16),
             pltpu.VMEM((rows, part, own), F32),
-            pltpu.VMEM((rows, chans // 2 - 1, 2, part, own), BF16),
+            pltpu.VMEM((rows, chans // 2 - 1, 2, folded, LANES), BF16),
             pltpu.VMEM((8, hid), F32),
             pltpu.VMEM((8, hid), F32),
             pltpu.VMEM(filter_in.shape, F32),
@@ -601,13 +697,14 @@
         ]
         + [pltpu.VMEM(t.shape, BF16) for t in tables]
         + [
+            pltpu.VMEM((part, chans * own), BF16),
             pltpu.VMEM((2, part, hid), BF16),
-            pltpu.SemaphoreType.DMA((8,)),
+            pltpu.SemaphoreType.DMA((7 + 2 * chans,)),
             pltpu.SemaphoreType.DMA((7, rows, peers)),
             pltpu.SemaphoreType.DMA((7, rows, peers)),
         ],
         compiler_params=pltpu.CompilerParams(
-            collective_id=0, has_side_effects=True, vmem_limit_bytes=48 * 1024 * 1024
+            collective_id=0, has_side_effects=True, vmem_limit_bytes=60 * 1024 * 1024
         ),
     )(*args)
     return result[None]
@@ -615,7 +712,9 @@
 
 def dispatch(sizes, *args):
     lats, chans = sizes["lat"], sizes["ch"]
-    if 2 * M // lats % 16 == 0 and chans > 2 and chans % 2 == 0:
+    own = args[0].shape[3]
+    folds = own // LANES == 1 and 2 * (own % LANES) == LANES
+    if folds and 2 * M // lats % 16 == 0 and chans > 2 and chans % 2 == 0:
         return fused(lats, chans, *args)
     return local(*args)
 

time: 152 us -> 139 us (0.914)
  Pallas kernels: 141 us -> 133 us
  local copies, waits for them, and re-layouts: 10.5 us -> 5.58 us
    pallas_call x1, Pallas kernels: 141 us -> 133 us  [fused(): pl.pallas_call(functools.partial(rollout, lats, chans), out_shape=jax.Sha...]
    unnamed x25 -> x1, local copies, waits for them, and re-layouts: 8.32 us -> 1.89 us
where the time goes in v1:
time: 139 us; the launch traced here: 138 us
  Pallas kernels  133 us (96%)
  local copies, waits for them, and re-layouts  5.58 us (4%)
    pallas_call x1, Pallas kernels, fused(): pl.pallas_call(functools.partial(rollout, lats, chans), out_shape=jax.Sha...  133 us

profile of v1, /device:TPU:0, one launch (start us, length us, event | category | flops | bytes accessed | tf_op | source)
XLA Modules:
  0.0 138.4 jit_solution(14271985652560971260)
XLA Ops:
  0.0 1.3 reshape.3.up_bias
  1.3 1.9 %copy.18 = f32[1,3,180,192]{3,2,0,1:T(8,128)} copy(f32[1,3,180,192]{3,0,2,1:T(1,128)} %param.14) | data formatting | bytes 829440
  3.1 132.8 %shard_map.136 = f32[3,180,192]{2,1,0:T(8,128)} custom-call(f32[3,180,192]{2,1,0:T(8,128)} %bitcast.5, bf16[2,192]{1,0:T(2,128)(2,1)} %gains.1, bf16[3,192]{1,0:T(4,128)(2,1)} %shifts.1, f32[2,2,96]{2,1,0:T(2,128)} %fin_bias.1, f32[2,2,96]{2,1,0:T(2,128)} %fout_bias.1, bf16[1,768]{1,0:T(2,128)(2,1)} %reshape.3.up_bias, f32[2,2,96,96]{3,2,1,0:T(8,128)} %fin_hbm.1, ...), custom_call_target="tpu_custom_call" | custom-call | tf_op jit(solution)/shard_map/pallas_call | solution.py:666
  136.0 2.4 %copy.15 = f32[1,3,180,192]{3,0,2,1:T(1,128)} copy(f32[1,3,180,192]{3,2,1,0:T(8,128)} %bitcast.4) | data formatting | bytes 829440 | tf_op jit(solution)/shard_map/broadcast_in_dim | solution.py:710

commit v2 on v1

--- a/solution.py
+++ b/solution.py
@@ -247,18 +247,18 @@
     target[where + (slice(rows, rows + rows // 2),)] = folded
 
 
-STAT, LON, ROW, STAT2, TOK, MIX, SETUP = range(7)
+STAT, LON, ROW, TOK, MIX, SETUP = range(6)
 
 
 def rollout(
     lats,
     chans,
-    state,
-    gains,
-    shifts,
-    fin_bias,
-    fout_bias,
-    up_bias,
+    state_hbm,
+    gains_hbm,
+    shifts_hbm,
+    fin_bias_hbm,
+    fout_bias_hbm,
+    up_bias_hbm,
     fin_hbm,
     fout_hbm,
     up_hbm,
@@ -267,7 +267,13 @@
     t_lat_hbm,
     t_rows_hbm,
     t_back_hbm,
-    out,
+    out_hbm,
+    state,
+    gains,
+    shifts,
+    fin_bias,
+    fout_bias,
+    up_bias,
     x,
     stat_send,
     stat_recv,
@@ -283,6 +289,9 @@
     mix_recv,
     bias_send,
     bias_recv,
+    par_send,
+    par_recv,
+    par,
     fin_raw,
     fout_raw,
     fin,
@@ -306,7 +315,7 @@
     lat, ch = lax.axis_index("lat"), lax.axis_index("ch")
     core, chip = lax.rem(ch, 2), lax.div(ch, 2)
     chips = chans // 2
-    rows, width, own = state.shape
+    rows, width, _, own = state.shape
     part = x.shape[2]
     near = -(-width // 2)
     wide = chans * own
@@ -325,13 +334,19 @@
         rest = own - LANES
         up_rows.append((pl.ds(c * own + LANES, rest), pl.ds(chans * LANES + c * rest, rest)))
 
-    lat_order = sorted(range(1, lats), reverse=True)
+    lat_order = sorted(range(1, lats), key=lambda k: -4 * (2 * k // lats) - 2 * (k % 2) - k / lats)
     ch_order = tuple(range(2, chans)) + (1,)
 
     loads = [
         pltpu.make_async_copy(source, target, load_sem.at[n])
         for n, (source, target) in enumerate(
             (
+                (state_hbm, state),
+                (gains_hbm, gains),
+                (shifts_hbm, shifts),
+                (up_bias_hbm, up_bias),
+                (fin_bias_hbm, fin_bias),
+                (fout_bias_hbm, fout_bias),
                 (fin_hbm, fin_raw),
                 (fout_hbm, fout_raw),
                 (t_lon_hbm, t_lon),
@@ -345,6 +360,9 @@
     ]
     for each in loads:
         each.start()
+    stores = [
+        pltpu.make_async_copy(state.at[r], out_hbm.at[r], load_sem.at[r]) for r in range(rows)
+    ]
 
     barrier = pltpu.get_barrier_semaphore()
     for k in lat_order:
@@ -362,10 +380,9 @@
             device_id_type=MESH,
         )
 
-    def stat_copies(kind, r):
-        n = kind // STAT2
+    def stat_copies(r):
         return [
-            copy(kind, r, q, stat_send.at[n, r], stat_recv.at[n, r, ch], {"ch": chan(q)})
+            copy(STAT, r, q, stat_send.at[r], stat_recv.at[r, ch], {"ch": chan(q)})
             for q in ch_order
         ]
 
@@ -387,13 +404,15 @@
             for q in ch_order
         ]
 
+    def mix_copy(r, q):
+        if q == 1:
+            return copy(MIX, r, q, mix_full.at[r, 1 - core], mix_pair.at[r], {"ch": chan(q)})
+        n = q // 2 - 1
+        source = mix_send.at[r, n, half_of(q)]
+        return copy(MIX, r, q, source, mix_recv.at[r, n, core], {"ch": chan(q)})
+
     def mix_copies(r):
-        copies = [
-            copy(MIX, r, q, mix_send.at[r, chan(q)], mix_recv.at[r, q // 2 - 1, core], {"ch": chan(q)})
-            for q in range(2, chans)
-        ]
-        copies.append(copy(MIX, r, 1, mix_full.at[r, chan(1)], mix_pair.at[r], {"ch": chan(1)}))
-        return copies
+        return [mix_copy(r, q) for q in ch_order]
 
     def start(copies):
         for each in copies:
@@ -403,13 +422,11 @@
         for each in copies:
             each.wait()
 
-    gain = gains[...].astype(F32)
-    shift = shifts[...].astype(F32)
-    bias_send[...] = jnp.broadcast_to(up_bias[...].astype(F32), bias_send.shape)
     x[...] = jnp.zeros_like(x)
+    loads[0].wait()
     for r in range(rows):
-        x[r, 0, 0:near] = state[r, 0:near]
-        x[r, 1, 0 : width - near] = state[r, near:width]
+        x[r, 0, 0:near] = state[r, 0:near, 0]
+        x[r, 1, 0 : width - near] = state[r, near:width, 0]
     ones = jnp.ones((8, own), BF16)
     which = lax.broadcasted_iota(jnp.int32, (8, 2 * part), 0)
 
@@ -420,29 +437,35 @@
             ones, high, dims, preferred_element_type=F32
         ) + lax.dot_general(ones, low, dims, preferred_element_type=F32)
 
-    def send_stats(kind, r):
-        n = kind // STAT2
+    def own_stats(r):
         values = x[r].reshape(2 * part, own)
         sums = jnp.where(which == 0, row_sums(values), row_sums(values * values))
-        stat_send[n, r] = sums
-        stat_recv[n, r, pl.ds(ch, 1)] = sums[None]
-        start(stat_copies(kind, r))
-
-    def take_stats(kind, r):
-        n = kind // STAT2
-        with jax.named_scope(f"wait_stat#n={n}"):
-            finish(stat_copies(kind, r))
-        total = stat_recv[n, r, 0]
+        stat_send[r] = sums
+        stat_recv[r, pl.ds(ch, 1)] = sums[None]
+
+    def take_stats(r):
+        with jax.named_scope("wait_stat"):
+            finish(stat_copies(r))
+        total = stat_recv[r, 0]
         for c in range(1, chans):
-            total = total + stat_recv[n, r, c]
+            total = total + stat_recv[r, c]
         mean = total[0:1] / wide
         scaled = lax.rsqrt(total[1:2] / wide - mean * mean + EPS)
         both = jnp.transpose(jnp.where(which == 0, mean, scaled))
         return both[:, 0:1], both[:, 1:2]
 
+    for r in range(rows):
+        own_stats(r)
     pl.semaphore_wait(barrier, lats + chans - 2)
     for r in range(rows):
-        send_stats(STAT, r)
+        start(stat_copies(r))
+    for each in loads[1:4]:
+        each.wait()
+    gain = gains[...].astype(F32)
+    shift = shifts[...].astype(F32)
+    par_send[...] = jnp.concatenate((gain[1:2], shift[1:2], jnp.zeros((6, own), F32)), 0)
+    par_recv[pl.ds(ch, 1)] = par_send[...][None]
+    bias_send[...] = jnp.broadcast_to(up_bias[...].astype(F32)[None], bias_send.shape)
     partner = {"ch": chan(1)}
     setup = [
         copy(SETUP, 0, 0, down_hbm, down_recv, partner),
@@ -452,9 +475,11 @@
         setup.append(
             copy(SETUP, 1 + n // chans, n % chans, up_hbm.at[source], up_recv.at[target], partner)
         )
+    for n, q in enumerate(ch_order):
+        setup.append(copy(SETUP, 0, 2 + n, par_send, par_recv.at[ch], {"ch": chan(q)}))
     start(setup)
-    loads[0].wait()
-    loads[1].wait()
+    for each in loads[4:8]:
+        each.wait()
     blocks, size = fin_raw.shape[1], fin_raw.shape[2]
     line = lax.broadcasted_iota(jnp.int32, (size, own), 0)
     lane = lax.broadcasted_iota(jnp.int32, (size, own), 1)
@@ -474,7 +499,7 @@
                 bias[:, n, :], shifted, precision=HIGH, preferred_element_type=F32
             )
         bias_target[...] = placed
-    for each in loads[2:6]:
+    for each in loads[8:12]:
         each.wait()
 
     def complex_apply(pair, weights, bias):
@@ -496,7 +521,7 @@
 
     def forward(r):
         with jax.named_scope("forward"):
-            mean, scaled = take_stats(STAT, r)
+            mean, scaled = take_stats(r)
             now = x[r].reshape(2 * part, own)
             normed = (now - mean) * scaled * gain[0:1] + shift[0:1]
             x[r] = (now + normed).reshape(2, part, own)
@@ -523,55 +548,69 @@
     def backward(r):
         data = spectrum(row_recv[r], share)
         back = dot(t_back[0], data) + dot(t_back[1], data)
-        x[r] = x[r] + back.reshape(2, part, own)
-        send_stats(STAT2, r)
-
-    def token(r):
-        mean, scaled = take_stats(STAT2, r)
-        now = x[r].reshape(2 * part, own)
-        normed = (now - mean) * scaled * gain[1:2] + shift[1:2]
-        store_packed(tok_send, (r, slice(None)), normed.reshape(2, part, own))
+        now = x[r] + back.reshape(2, part, own)
+        x[r] = now
+        store_packed(tok_send, (r, slice(None)), now)
         start(tok_copies(r))
         tok_recv[r, pl.ds(ch, 1)] = tok_send[r, pl.ds(core, 1)]
 
+    def token_piece(r, n):
+        if n < chans:
+            return tok_recv[r, n, 0:part].astype(F32)
+        c = 2 * (n - chans)
+        one = tok_recv[r, c, part : part + part // 2].astype(F32)
+        two = tok_recv[r, c + 1, part : part + part // 2].astype(F32)
+        rest = LANES // 2
+        upper = jnp.concatenate((one[:, :rest], two[:, :rest]), -1)
+        lower = jnp.concatenate((one[:, rest:], two[:, rest:]), -1)
+        return jnp.concatenate((upper, lower), 0)
+
     def project_up(r):
-        for c in range(chans):
-            tokens[:, c * LANES : (c + 1) * LANES] = tok_recv[r, c, 0:part]
-        middle = part // 2
-        for c in range(0, chans, 2):
-            cut = slice((chans + c // 2) * LANES, (chans + c // 2 + 1) * LANES)
-            one = tok_recv[r, c, part : part + middle]
-            two = tok_recv[r, c + 1, part : part + middle]
-            for n, lanes in enumerate((slice(0, LANES // 2), slice(LANES // 2, LANES))):
-                pair = jnp.concatenate((one[:, lanes], two[:, lanes]), -1)
-                tokens[n * middle : (n + 1) * middle, cut] = pair
+        total, squares = 0.0, 0.0
+        for n in range(wide // LANES):
+            piece = token_piece(r, n)
+            total = total + piece
+            squares = squares + piece * piece
+        mean = jnp.sum(total, -1, keepdims=True) / wide
+        spread = jnp.sum(squares, -1, keepdims=True) / wide - mean * mean
+        scaled = lax.rsqrt(spread + EPS)
+        for n in range(wide // LANES):
+            cut = slice(n * LANES, (n + 1) * LANES)
+            normed = (token_piece(r, n) - mean) * scaled * par[0:1, cut] + par[1:2, cut]
+            tokens[0:part, cut], tokens[part : 2 * part, cut] = halves(normed)
         for s, (weight, bias) in enumerate(((up, bias_send), (up_recv, bias_recv))):
             for lo in range(0, hid, 256):
                 cut = slice(lo, lo + 256)
-                pre = dot(tokens[...], weight[:, cut]) + bias[0:1, cut]
+                both = dot(tokens[...], weight[:, cut])
+                pre = both[:part] + both[part:] + bias[0:1, cut]
                 hidden[s, :, cut] = gelu(pre).astype(BF16)
 
     def project_down(r):
-        mixed = dot(hidden[0], down[...]) + dot(hidden[1], down_recv[...])
-        for c in range(chans):
-            piece = mixed[:, c * own : (c + 1) * own]
-            mix_full[r, c] = piece
-            store_packed(mix_send, (r, c), piece)
-        start(mix_copies(r))
+        for j in tuple(range(1, chips)) + (0,):
+            first = pl.multiple_of(2 * own * lax.rem(chip + j, chips), LANES)
+            cut = pl.ds(first, 2 * own)
+            mixed = dot(hidden[0], down[:, cut]) + dot(hidden[1], down_recv[:, cut])
+            for n in range(2):
+                piece = mixed[:, n * own : (n + 1) * own]
+                if j:
+                    store_packed(mix_send, (r, j - 1, n), piece)
+                else:
+                    mix_full[r, n] = piece
+            for q in (2 * j, 2 * j + 1):
+                if q:
+                    mix_copy(r, q).start()
 
     def residual(r):
-        for h, piece in ((core, mix_full[r, pl.ds(ch, 1)]), (1 - core, mix_pair[r][None])):
+        for h, piece in ((core, mix_full[r, pl.ds(core, 1)]), (1 - core, mix_pair[r][None])):
             for n in range(chips - 1):
                 message = mix_recv[r, n, pl.ds(h, 1)]
                 rest = unfold(message[:, part:])
                 piece = piece + jnp.concatenate((message[:, :part].astype(F32), rest), -1)
             x[r, pl.ds(h, 1)] = x[r, pl.ds(h, 1)] + piece + shift[2:3]
 
-    forward(0)
-
     @pl.loop(0, STEPS)
     def _(index):
-        for r in range(1, rows):
+        for r in range(rows):
             forward(r)
         with jax.named_scope("wait_lon"):
             for r in range(rows):
@@ -586,15 +625,15 @@
                 finish(row_copies(r))
             with jax.named_scope("backward"):
                 backward(r)
-        for r in range(rows):
-            with jax.named_scope("token"):
-                token(r)
 
         @pl.when(index == 0)
         def _():
-            for each in loads[6:]:
+            for each in loads[12:]:
                 each.wait()
             finish(setup)
+            pieces = [par_recv[c, 0:2, :LANES] for c in range(chans)]
+            pieces += [par_recv[c, 0:2, LANES:] for c in range(chans)]
+            par[...] = jnp.concatenate(pieces, -1)
 
         for r in range(rows):
             with jax.named_scope("wait_tok"):
@@ -604,24 +643,24 @@
             with jax.named_scope("down"):
                 project_down(r)
         for r in range(rows):
-            if r == rows - 1:
-
-                @pl.when(index < STEPS - 1)
-                def _():
-                    forward(0)
-
             with jax.named_scope("wait_mix"):
                 finish(mix_copies(r))
             with jax.named_scope("residual"):
                 residual(r)
 
+            @pl.when(index == STEPS - 1)
+            def _():
+                state[r, 0:near, 0] = x[r, 0, 0:near]
+                state[r, near:width, 0] = x[r, 1, 0 : width - near]
+                stores[r].start()
+
             @pl.when(index < STEPS - 1)
             def _():
-                send_stats(STAT, r)
-
-    for r in range(rows):
-        out[r, 0:near] = x[r, 0, 0:near]
-        out[r, near:width] = x[r, 1, 0 : width - near]
+                own_stats(r)
+                start(stat_copies(r))
+
+    for each in stores:
+        each.wait()
 
 
 def fused(
@@ -646,18 +685,17 @@
         jnp.asarray(t) for t in fourier_tables(width, part, rows * lats, M, lats)
     )
     args = (
-        state[0],
+        state.transpose(1, 2, 0, 3),
         norm_gains,
         channel_biases,
         filter_in_bias,
         filter_out_bias,
-        up_bias.reshape(1, hid),
+        up_bias,
         filter_in,
         filter_out,
         up_weight,
         down_weight,
     ) + tables
-    vmem = pl.BlockSpec(memory_space=pltpu.VMEM)
     hbm = pl.BlockSpec(memory_space=pltpu.HBM)
     packed = share + share // 2
     spectrum = (rows, lats, packed, LANES)
@@ -665,25 +703,34 @@
     peers = max(lats, chans)
     result = pl.pallas_call(
         functools.partial(rollout, lats, chans),
-        out_shape=jax.ShapeDtypeStruct((rows, width, own), F32),
-        in_specs=[vmem] * 6 + [hbm] * 8,
-        out_specs=vmem,
+        out_shape=jax.ShapeDtypeStruct((rows, width, 1, own), F32),
+        in_specs=[hbm] * 14,
+        out_specs=hbm,
         scratch_shapes=[
+            pltpu.VMEM((rows, width, 1, own), F32),
+            pltpu.VMEM(norm_gains.shape, BF16),
+            pltpu.VMEM(channel_biases.shape, BF16),
+            pltpu.VMEM(filter_in_bias.shape, F32),
+            pltpu.VMEM(filter_out_bias.shape, F32),
+            pltpu.VMEM(up_bias.shape, BF16),
             pltpu.VMEM((rows, 2, part, own), F32),
-            pltpu.VMEM((2, rows, 8, 2 * part), F32),
-            pltpu.VMEM((2, rows, chans, 8, 2 * part), F32),
+            pltpu.VMEM((rows, 8, 2 * part), F32),
+            pltpu.VMEM((rows, chans, 8, 2 * part), F32),
             pltpu.VMEM(spectrum, BF16),
             pltpu.VMEM((lats, rows, packed, LANES), BF16),
             pltpu.VMEM(spectrum, BF16),
             pltpu.VMEM(spectrum, BF16),
             pltpu.VMEM((rows, 2, folded, LANES), BF16),
             pltpu.VMEM((rows, chans, folded, LANES), BF16),
-            pltpu.VMEM((rows, chans, part, own), F32),
-            pltpu.VMEM((rows, chans, folded, LANES), BF16),
+            pltpu.VMEM((rows, 2, part, own), F32),
+            pltpu.VMEM((rows, chans // 2 - 1, 2, folded, LANES), BF16),
             pltpu.VMEM((rows, part, own), F32),
             pltpu.VMEM((rows, chans // 2 - 1, 2, folded, LANES), BF16),
             pltpu.VMEM((8, hid), F32),
             pltpu.VMEM((8, hid), F32),
+            pltpu.VMEM((8, own), F32),
+            pltpu.VMEM((chans, 8, own), F32),
+            pltpu.VMEM((2, chans * own), F32),
             pltpu.VMEM(filter_in.shape, F32),
             pltpu.VMEM(filter_out.shape, F32),
             pltpu.VMEM((2, 2, own, own), BF16),
@@ -697,17 +744,17 @@
         ]
         + [pltpu.VMEM(t.shape, BF16) for t in tables]
         + [
-            pltpu.VMEM((part, chans * own), BF16),
+            pltpu.VMEM((2 * part, chans * own), BF16),
             pltpu.VMEM((2, part, hid), BF16),
-            pltpu.SemaphoreType.DMA((7 + 2 * chans,)),
-            pltpu.SemaphoreType.DMA((7, rows, peers)),
-            pltpu.SemaphoreType.DMA((7, rows, peers)),
+            pltpu.SemaphoreType.DMA((13 + 2 * chans,)),
+            pltpu.SemaphoreType.DMA((6, max(rows, 3), peers)),
+            pltpu.SemaphoreType.DMA((6, max(rows, 3), peers)),
         ],
         compiler_params=pltpu.CompilerParams(
             collective_id=0, has_side_effects=True, vmem_limit_bytes=60 * 1024 * 1024
         ),
     )(*args)
-    return result[None]
+    return result.transpose(2, 0, 1, 3)
 
 
 def dispatch(sizes, *args):

time: 139 us -> 115 us (0.83)
  Pallas kernels: 133 us -> 112 us
  local copies, waits for them, and re-layouts: 5.58 us -> 2.23 us
    pallas_call x1, Pallas kernels: 133 us -> 112 us  [fused(): pl.pallas_call(functools.partial(rollout, lats, chans), out_shape=jax.Sha...]
    broadcast_in_dim x1 -> x0, local copies, waits for them, and re-layouts: 2.43 us -> none  [fused(): return result[None]]
where the time goes in v2:
time: 115 us; the launch traced here: 114 us
  Pallas kernels  112 us (97%)
  local copies, waits for them, and re-layouts  2.23 us (2%)
    pallas_call x1, Pallas kernels, fused(): pl.pallas_call(functools.partial(rollout, lats, chans), out_shape=jax.Sha...  112 us

profile of v2, /device:TPU:0, one launch (start us, length us, event | category | flops | bytes accessed | tf_op | source)
XLA Modules:
  0.0 114.4 jit_solution(9900334452126121800)
XLA Ops:
  0.0 112.1 %shard_map.136 = f32[3,180,1,192]{3,2,1,0:T(1,128)} custom-call(f32[3,180,1,192]{3,2,1,0:T(1,128)} %bitcast.3, bf16[2,192]{1,0:T(2,128)(2,1)} %gains_hbm.1, bf16[3,192]{1,0:T(4,128)(2,1)} %shifts_hbm.1, f32[2,2,96]{2,1,0:T(2,128)} %fin_bias_hbm.1, f32[2,2,96]{2,1,0:T(2,128)} %fout_bias_hbm.1, bf16[768]{0:T(1024)(128)(2,1)} %up_bias_hbm.1, ...), custom_call_target="tpu_custom_call" | custom-call | tf_op jit(solution)/shard_map/pallas_call | solution.py:704
  112.1 2.2 %copy.16 = f32[1,3,180,192]{3,0,2,1:T(1,128)} copy(f32[1,3,180,192]{3,0,2,1:T(1,128)} %bitcast.2) | data formatting | bytes 829440

commit v3 on v2

--- a/solution.py
+++ b/solution.py
@@ -440,8 +440,8 @@
     def own_stats(r):
         values = x[r].reshape(2 * part, own)
         sums = jnp.where(which == 0, row_sums(values), row_sums(values * values))
-        stat_send[r] = sums
-        stat_recv[r, pl.ds(ch, 1)] = sums[None]
+        stat_send[r] = sums[0:2]
+        stat_recv[r, pl.ds(ch, 1)] = sums[None, 0:2]
 
     def take_stats(r):
         with jax.named_scope("wait_stat"):
@@ -532,16 +532,25 @@
 
     def spectral():
         data = spectrum(lon_recv[...], share)
-        spec = dot(t_lat[0], data) + dot(t_lat[1], data)
+        size = t_lat.shape[1] // 4
+        spec = []
+        for n in range(4):
+            cut = slice(n * size, (n + 1) * size)
+            spec.append(dot(t_lat[0, cut], data) + dot(t_lat[1, cut], data))
+        spec = jnp.concatenate(spec, 0)
         real, imag = complex_apply(spec, fin, fin_b)
         pair = jnp.concatenate((jnp.maximum(real, 0.0), jnp.maximum(imag, 0.0)), 0)
         real, imag = complex_apply(pair, fout, fout_b)
         return halves(jnp.concatenate((soft_shrink(real), soft_shrink(imag)), 0))
 
     def unmix(r, pair):
-        cut = slice(r * spread_modes, (r + 1) * spread_modes)
-        back = dot3((t_rows[0, cut], t_rows[1, cut]), pair)
-        store_packed(row_send, (r, slice(None)), back.reshape(lats, share, own))
+        count = spread_modes // 2
+        for n in range(2):
+            first = r * spread_modes + n * count
+            cut = slice(first, first + count)
+            back = dot3((t_rows[0, cut], t_rows[1, cut]), pair)
+            where = (r, slice(n * lats // 2, (n + 1) * lats // 2))
+            store_packed(row_send, where, back.reshape(lats // 2, share, own))
         start(row_copies(r))
         row_recv[r, pl.ds(lat, 1)] = row_send[r, pl.ds(lat, 1)]
 
@@ -565,7 +574,7 @@
         lower = jnp.concatenate((one[:, rest:], two[:, rest:]), -1)
         return jnp.concatenate((upper, lower), 0)
 
-    def project_up(r):
+    def normalize(r):
         total, squares = 0.0, 0.0
         for n in range(wide // LANES):
             piece = token_piece(r, n)
@@ -577,11 +586,13 @@
         for n in range(wide // LANES):
             cut = slice(n * LANES, (n + 1) * LANES)
             normed = (token_piece(r, n) - mean) * scaled * par[0:1, cut] + par[1:2, cut]
-            tokens[0:part, cut], tokens[part : 2 * part, cut] = halves(normed)
+            tokens[r % 2, 0:part, cut], tokens[r % 2, part : 2 * part, cut] = halves(normed)
+
+    def project_up(r):
         for s, (weight, bias) in enumerate(((up, bias_send), (up_recv, bias_recv))):
             for lo in range(0, hid, 256):
                 cut = slice(lo, lo + 256)
-                both = dot(tokens[...], weight[:, cut])
+                both = dot(tokens[r % 2], weight[:, cut])
                 pre = both[:part] + both[part:] + bias[0:1, cut]
                 hidden[s, :, cut] = gelu(pre).astype(BF16)
 
@@ -636,11 +647,19 @@
             par[...] = jnp.concatenate(pieces, -1)
 
         for r in range(rows):
-            with jax.named_scope("wait_tok"):
-                finish(tok_copies(r))
+            if r <= 1:
+                with jax.named_scope("wait_tok"):
+                    finish(tok_copies(r))
+                with jax.named_scope("norm"):
+                    normalize(r)
             with jax.named_scope("up"):
                 project_up(r)
+            if 1 <= r < rows - 1:
+                with jax.named_scope("wait_tok"):
+                    finish(tok_copies(r + 1))
             with jax.named_scope("down"):
+                if 1 <= r < rows - 1:
+                    normalize(r + 1)
                 project_down(r)
         for r in range(rows):
             with jax.named_scope("wait_mix"):
@@ -714,8 +733,8 @@
             pltpu.VMEM(filter_out_bias.shape, F32),
             pltpu.VMEM(up_bias.shape, BF16),
             pltpu.VMEM((rows, 2, part, own), F32),
-            pltpu.VMEM((rows, 8, 2 * part), F32),
-            pltpu.VMEM((rows, chans, 8, 2 * part), F32),
+            pltpu.VMEM((rows, 2, 2 * part), F32),
+            pltpu.VMEM((rows, chans, 2, 2 * part), F32),
             pltpu.VMEM(spectrum, BF16),
             pltpu.VMEM((lats, rows, packed, LANES), BF16),
             pltpu.VMEM(spectrum, BF16),
@@ -744,7 +763,7 @@
         ]
         + [pltpu.VMEM(t.shape, BF16) for t in tables]
         + [
-            pltpu.VMEM((2 * part, chans * own), BF16),
+            pltpu.VMEM((2, 2 * part, chans * own), BF16),
             pltpu.VMEM((2, part, hid), BF16),
             pltpu.SemaphoreType.DMA((13 + 2 * chans,)),
             pltpu.SemaphoreType.DMA((6, max(rows, 3), peers)),

time: 115 us -> 113 us (0.983)
  no operation moved by 1% of the time
where the time goes in v3:
time: 113 us
  Pallas kernels  111 us (98%)
  local copies, waits for them, and re-layouts  2.23 us (2%)
    pallas_call x1, Pallas kernels, fused(): pl.pallas_call(functools.partial(rollout, lats, chans), out_shape=jax.Sha...  111 us

profile of v3, /device:TPU:0, one launch (start us, length us, event | category | flops | bytes accessed | tf_op | source)
XLA Modules:
  0.0 113.3 jit_solution(4147410395111408558)
XLA Ops:
  0.0 111.1 %shard_map.136 = f32[3,180,1,192]{3,2,1,0:T(1,128)} custom-call(f32[3,180,1,192]{3,2,1,0:T(1,128)} %bitcast.3, bf16[2,192]{1,0:T(2,128)(2,1)} %gains_hbm.1, bf16[3,192]{1,0:T(4,128)(2,1)} %shifts_hbm.1, f32[2,2,96]{2,1,0:T(2,128)} %fin_bias_hbm.1, f32[2,2,96]{2,1,0:T(2,128)} %fout_bias_hbm.1, bf16[768]{0:T(1024)(128)(2,1)} %up_bias_hbm.1, ...), custom_call_target="tpu_custom_call" | custom-call | tf_op jit(solution)/shard_map/pallas_call | solution.py:723
  111.1 2.2 %copy.16 = f32[1,3,180,192]{3,0,2,1:T(1,128)} copy(f32[1,3,180,192]{3,0,2,1:T(1,128)} %bitcast.2) | data formatting | bytes 829440

commit v4 on v3

--- a/solution.py
+++ b/solution.py
@@ -682,6 +682,19 @@
         each.wait()
 
 
+def hand_over(source, target, held, read_sem, write_sem):
+    rows = source.shape[0]
+    reads = [pltpu.make_async_copy(source.at[r], held.at[r], read_sem.at[r]) for r in range(rows)]
+    writes = [pltpu.make_async_copy(held.at[r], target.at[r], write_sem.at[r]) for r in range(rows)]
+    for each in reads:
+        each.start()
+    for read, write in zip(reads, writes):
+        read.wait()
+        write.start()
+    for each in writes:
+        each.wait()
+
+
 def fused(
     lats,
     chans,
@@ -773,6 +786,18 @@
             collective_id=0, has_side_effects=True, vmem_limit_bytes=60 * 1024 * 1024
         ),
     )(*args)
+    result = pl.pallas_call(
+        hand_over,
+        out_shape=jax.ShapeDtypeStruct(result.shape, F32),
+        in_specs=[hbm],
+        out_specs=hbm,
+        scratch_shapes=[
+            pltpu.VMEM(result.shape, F32),
+            pltpu.SemaphoreType.DMA((rows,)),
+            pltpu.SemaphoreType.DMA((rows,)),
+        ],
+        compiler_params=pltpu.CompilerParams(vmem_limit_bytes=60 * 1024 * 1024),
+    )(result)
     return result.transpose(2, 0, 1, 3)
 
 

time: 113 us -> 113 us (level)
  local copies, waits for them, and re-layouts: 2.23 us -> 0 us
  Pallas kernels: 111 us -> 113 us
    unnamed x1 -> x0, local copies, waits for them, and re-layouts: 2.23 us -> none
    pallas_call x0 -> x1, Pallas kernels: none -> 1.82 us  [fused(): pl.pallas_call(hand_over, out_shape=jax.ShapeDtypeStruct(result.shape, F3...]
where the time goes in v4:
time: 113 us
  Pallas kernels  113 us (100%)
    pallas_call x1, Pallas kernels, fused(): pl.pallas_call(functools.partial(rollout, lats, chans), out_shape=jax.Sha...  111 us

profile of v4, /device:TPU:0, one launch (start us, length us, event | category | flops | bytes accessed | tf_op | source)
XLA Modules:
  0.0 112.9 jit_solution(5450336409438864124)
XLA Ops:
  0.0 111.1 %shard_map.136.source = f32[3,180,1,192]{3,2,1,0:T(1,128)} custom-call(f32[3,180,1,192]{3,2,1,0:T(1,128)} %bitcast.2, bf16[2,192]{1,0:T(2,128)(2,1)} %gains_hbm.1, bf16[3,192]{1,0:T(4,128)(2,1)} %shifts_hbm.1, f32[2,2,96]{2,1,0:T(2,128)} %fin_bias_hbm.1, f32[2,2,96]{2,1,0:T(2,128)} %fout_bias_hbm.1, bf16[768]{0:T(1024)(128)(2,1)} %up_bias_hbm.1, ...), custom_call_target="tpu_custom_call" | custom-call | tf_op jit(solution)/shard_map/pallas_call | solution.py:736
  111.1 1.8 %shard_map.137 = f32[3,180,1,192]{3,2,1,0:T(1,128)} custom-call(f32[3,180,1,192]{3,2,1,0:T(1,128)} %shard_map.136.source), custom_call_target="tpu_custom_call" | custom-call | tf_op jit(solution)/shard_map/pallas_call | solution.py:789

commit v5 on v4

--- a/solution.py
+++ b/solution.py
@@ -283,6 +283,7 @@
     row_recv,
     tok_send,
     tok_recv,
+    tok_pair,
     mix_full,
     mix_send,
     mix_pair,
@@ -328,11 +329,21 @@
     def half_of(q):
         return core if q % 2 == 0 else 1 - core
 
-    up_rows = []
-    for c in range(chans):
-        up_rows.append((pl.ds(c * own, LANES), pl.ds(c * LANES, LANES)))
+    others = [2 * lax.rem(chip + j, chips) + n for j in range(1, chips) for n in range(2)]
+
+    def slot_rows(order):
         rest = own - LANES
-        up_rows.append((pl.ds(c * own + LANES, rest), pl.ds(chans * LANES + c * rest, rest)))
+        pairs = []
+        for n, c in enumerate(order):
+            first = pl.multiple_of(c * own, rest)
+            then = pl.multiple_of(c * own + LANES, rest)
+            pairs.append((pl.ds(first, LANES), pl.ds(n * LANES, LANES)))
+            pairs.append((pl.ds(then, rest), pl.ds(chans * LANES + n * rest, rest)))
+        return pairs
+
+    order = [ch, chan(1)] + others
+    up_rows = slot_rows(order)
+    partner_rows = slot_rows([chan(1), ch] + others)
 
     lat_order = sorted(range(1, lats), key=lambda k: -4 * (2 * k // lats) - 2 * (k % 2) - k / lats)
     ch_order = tuple(range(2, chans)) + (1,)
@@ -399,10 +410,13 @@
         ]
 
     def tok_copies(r):
-        return [
-            copy(TOK, r, q, tok_send.at[r, half_of(q)], tok_recv.at[r, ch], {"ch": chan(q)})
-            for q in ch_order
-        ]
+        copies = []
+        for q in range(2, chans):
+            slot = 2 * ((chips - q // 2) % chips - 1) + core
+            source = tok_send.at[r, half_of(q)]
+            copies.append(copy(TOK, r, q, source, tok_recv.at[r, slot], {"ch": chan(q)}))
+        copies.append(copy(TOK, r, 1, x.at[r, 1 - core], tok_pair.at[r], {"ch": chan(1)}))
+        return copies
 
     def mix_copy(r, q):
         if q == 1:
@@ -471,7 +485,7 @@
         copy(SETUP, 0, 0, down_hbm, down_recv, partner),
         copy(SETUP, 0, 1, bias_send, bias_recv, partner),
     ]
-    for n, (source, target) in enumerate(up_rows):
+    for n, (source, target) in enumerate(partner_rows):
         setup.append(
             copy(SETUP, 1 + n // chans, n % chans, up_hbm.at[source], up_recv.at[target], partner)
         )
@@ -561,12 +575,18 @@
         x[r] = now
         store_packed(tok_send, (r, slice(None)), now)
         start(tok_copies(r))
-        tok_recv[r, pl.ds(ch, 1)] = tok_send[r, pl.ds(core, 1)]
 
     def token_piece(r, n):
+        if n == 0:
+            return x[r, pl.ds(core, 1), :, :LANES][0]
+        if n == 1:
+            return tok_pair[r, :, :LANES]
+        if n == chans:
+            mine = x[r, pl.ds(core, 1), :, LANES:][0]
+            return jnp.concatenate((mine, tok_pair[r, :, LANES:]), -1)
         if n < chans:
-            return tok_recv[r, n, 0:part].astype(F32)
-        c = 2 * (n - chans)
+            return tok_recv[r, n - 2, 0:part].astype(F32)
+        c = 2 * (n - chans - 1)
         one = tok_recv[r, c, part : part + part // 2].astype(F32)
         two = tok_recv[r, c + 1, part : part + part // 2].astype(F32)
         rest = LANES // 2
@@ -586,7 +606,10 @@
         for n in range(wide // LANES):
             cut = slice(n * LANES, (n + 1) * LANES)
             normed = (token_piece(r, n) - mean) * scaled * par[0:1, cut] + par[1:2, cut]
-            tokens[r % 2, 0:part, cut], tokens[r % 2, part : 2 * part, cut] = halves(normed)
+            high, low = halves(normed)
+            tokens[r % 2, 0:part, cut] = high
+            near = n in (0, 1, chans)
+            tokens[r % 2, part : 2 * part, cut] = jnp.zeros_like(low) if near else low
 
     def project_up(r):
         for s, (weight, bias) in enumerate(((up, bias_send), (up_recv, bias_recv))):
@@ -642,8 +665,8 @@
             for each in loads[12:]:
                 each.wait()
             finish(setup)
-            pieces = [par_recv[c, 0:2, :LANES] for c in range(chans)]
-            pieces += [par_recv[c, 0:2, LANES:] for c in range(chans)]
+            pieces = [par_recv[c, 0:2, :LANES] for c in order]
+            pieces += [par_recv[c, 0:2, LANES:] for c in order]
             par[...] = jnp.concatenate(pieces, -1)
 
         for r in range(rows):
@@ -753,7 +776,8 @@
             pltpu.VMEM(spectrum, BF16),
             pltpu.VMEM(spectrum, BF16),
             pltpu.VMEM((rows, 2, folded, LANES), BF16),
-            pltpu.VMEM((rows, chans, folded, LANES), BF16),
+            pltpu.VMEM((rows, chans - 2, folded, LANES), BF16),
+            pltpu.VMEM((rows, part, own), F32),
             pltpu.VMEM((rows, 2, part, own), F32),
             pltpu.VMEM((rows, chans // 2 - 1, 2, folded, LANES), BF16),
             pltpu.VMEM((rows, part, own), F32),

time: 113 us -> 113 us (level)
  no operation moved by 1% of the time
where the time goes in v5:
time: 113 us
  Pallas kernels  113 us (100%)
    pallas_call x1, Pallas kernels, fused(): pl.pallas_call(functools.partial(rollout, lats, chans), out_shape=jax.Sha...  111 us

profile of v5, /device:TPU:0, one launch (start us, length us, event | category | flops | bytes accessed | tf_op | source)
XLA Modules:
  0.0 112.9 jit_solution(11850592810548094255)
XLA Ops:
  0.0 111.1 %shard_map.136.source = f32[3,180,1,192]{3,2,1,0:T(1,128)} custom-call(f32[3,180,1,192]{3,2,1,0:T(1,128)} %bitcast.2, bf16[2,192]{1,0:T(2,128)(2,1)} %gains_hbm.1, bf16[3,192]{1,0:T(4,128)(2,1)} %shifts_hbm.1, f32[2,2,96]{2,1,0:T(2,128)} %fin_bias_hbm.1, f32[2,2,96]{2,1,0:T(2,128)} %fout_bias_hbm.1, bf16[768]{0:T(1024)(128)(2,1)} %up_bias_hbm.1, ...), custom_call_target="tpu_custom_call" | custom-call | tf_op jit(solution)/shard_map/pallas_call | solution.py:759
  111.1 1.8 %shard_map.137 = f32[3,180,1,192]{3,2,1,0:T(1,128)} custom-call(f32[3,180,1,192]{3,2,1,0:T(1,128)} %shard_map.136.source), custom_call_target="tpu_custom_call" | custom-call | tf_op jit(solution)/shard_map/pallas_call | solution.py:813
